TPU v7x, 512 devices: a whole 4x8x8 slice. The times are simulated.
512 devices in a mesh: pair: 2 (over y_lo), dp: 32 (over x, z), ep: 8 (over y_hi, core).
Axes of the slice: x: 4, y: 8 (y_hi: 4, y_lo: 2; y = y_hi * 2 + y_lo), z: 8, core: 2. Of those that a mesh axis runs over, the one named last changes fastest.
Arguments:
- activations: bfloat16 [49152, 4096], P(('pair', 'dp'), 'ep'), parts along dimension 1, may hold values from -16 to 16
- cotangents: bfloat16 [49152, 16384], P(('pair', 'dp'), 'ep'), parts along dimension 1, may hold values from -1.75 to 1.75
Outputs:
- averaged_grad: bfloat16 [512, 16384], P('pair', 'ep'), parts along dimension 1
There are 8 independent parts, one for each index of `ep`. A program takes and returns all parts, laid end to end along the dimension named above; each array names one. Nothing has to cross between parts.
All inputs are finite; a program needn't handle non-finite values.
Results may differ from a plain program's by a relative error of at most 0.001.
Values may be sent and summed in bfloat16 or wider, within the bound.
A program may use at most 64 MiB of HBM per device.

v0:
```python
import jax
import jax.numpy as jnp
from jax import lax
from jax.sharding import Mesh
from jax.sharding import PartitionSpec as P

DP = ("dp_0", "dp_1")
PAIR_DP = ("pair", "dp_0", "dp_1")


def rows_for(lines, peers):
    spare = -len(lines) % peers
    return jnp.pad(lines, [(0, spare)] + [(0, 0)] * (lines.ndim - 1))


def copy_for_each(x, axis):
    copies = jnp.broadcast_to(x, (lax.axis_size(axis), *x.shape))
    return lax.all_to_all(copies, axis, split_axis=0, concat_axis=0, tiled=True)


def in_order(parts, dim):
    parts = jnp.moveaxis(parts, 0, dim)
    shape = parts.shape
    return parts.reshape(*shape[:dim], shape[dim] * shape[dim + 1], *shape[dim + 2 :])


def gathered_by_axis(x, axes, dim):
    far, near = axes
    leading = copy_for_each(x, far)
    parts = jnp.swapaxes(copy_for_each(leading, near), 0, 1)
    return in_order(parts.reshape(-1, *x.shape), dim)


def split_up(x, dim, peers):
    shape = x.shape
    parts = x.reshape(*shape[:dim], peers, shape[dim] // peers, *shape[dim + 1 :])
    return jnp.moveaxis(parts, dim, 0)


def summed_on_arrival(x, axis, dim):
    peers = lax.axis_size(axis)
    parts = lax.all_to_all(split_up(x, dim, peers), axis, 0, 0, tiled=True)
    return jnp.sum(parts, axis=0)


def sum_by_axis(x, axes, dim):
    far, near = axes
    parts = split_up(x, dim, lax.axis_size(far))
    nearer = summed_on_arrival(parts, near, dim + 1)
    arrived = lax.all_to_all(nearer, far, split_axis=0, concat_axis=0, tiled=True)
    return arrived.sum(axis=0)


def nested_sum(x, axes):
    lines = x.reshape(-1, x.shape[-1])
    padded = rows_for(lines, lax.axis_size(axes[0]) * lax.axis_size(axes[1]))
    whole = gathered_by_axis(sum_by_axis(padded, axes, 0), axes, 0)
    return lax.slice_in_dim(whole, 0, len(lines)).reshape(x.shape)


def local(activations, cotangents):
    replicas = lax.axis_size("pair") * lax.axis_size(DP)
    partial_grad = lax.dot_general(
        activations, cotangents, (((0,), (0,)), ((), ())), preferred_element_type=jnp.float32
    )
    grad_total = nested_sum(partial_grad, ("pair", ("dp_0", "dp_1")))
    half_rows = activations.shape[1] // lax.axis_size("pair")
    own_rows = lax.dynamic_slice_in_dim(
        grad_total, lax.axis_index("pair") * half_rows, half_rows, 0
    )
    return (own_rows / replicas).astype(jnp.bfloat16)


def solution(mesh):
    split = Mesh(
        mesh.devices.reshape(mesh.shape["pair"], 4, 8, mesh.shape["ep"]),
        ("pair", "dp_0", "dp_1", "ep"),
    )
    placed = (P(PAIR_DP, "ep"), P(PAIR_DP, "ep"))
    return jax.shard_map(
        local, mesh=split, in_specs=placed, out_specs=P("pair", "ep"), check_vma=False
    )
```

profile of v0, /device:TPU:32, one launch (start us, length us, event | category | flops | bytes accessed | tf_op | source)
XLA Modules:
  0.0 236.1 jit_solution(15673615468565433974)
XLA Ops:
  0.0 0.0 copy-start
  0.0 1.9 copy-done
  1.9 3.0 %fusion = f32[512,2048]{1,0:T(8,128)S(1)} fusion(bf16[768,512]{1,0:T(8,128)(2,1)} %param.2, bf16[768,2048]{1,0:T(8,128)(2,1)S(1)} %copy-done), kind=kOutput, calls=%fused_computation.2 | convolution fusion | flops 1610612736 | bytes 8126464 | tf_op jit(solution)/shard_map/dot_general | solution.py:63
  4.9 0.5 copy.9
  5.3 109.2 %all_to_all.20 = f32[32,2,8,2048]{3,2,1,0:T(8,128)} all-to-all(f32[32,2,8,2048]{3,2,1,0:T(8,128)S(1)} %bitcast.9), channel_id=1, replica_groups=mesh['pair'=2,'dp_0'=4,'dp_1'=8,'ep'=8] {'dp_0','dp_1'}, dimensions={0} | all-to-all | bytes 8388608 | tf_op jit(solution)/shard_map/all_to_all | solution.py:42
  114.6 2.4 %reduce_sum.18 = f32[2,8,2048]{2,1,0:T(8,128)S(1)} reduce(f32[32,2,8,2048]{3,2,1,0:T(8,128)} %all_to_all.20, f32[]{:T(128)} %constant.3.clone.1), dimensions={0}, to_apply=%region_0.1 | reduce | flops 1015808 | bytes 4325380 | tf_op jit(solution)/shard_map/reduce_sum | solution.py:43
  117.0 7.5 %all_to_all.21 = f32[2,8,2048]{2,1,0:T(8,128)S(1)} all-to-all(f32[2,8,2048]{2,1,0:T(8,128)S(1)} %reduce_sum.18), channel_id=1, replica_groups=mesh['pair'=2,'dp_0'=4,'dp_1'=8,'ep'=8] {'pair'}, dimensions={0} | all-to-all | bytes 262144 | tf_op jit(solution)/shard_map/all_to_all | solution.py:50
  124.5 6.8 %all_to_all.22 = f32[2,8,2048]{2,1,0:T(8,128)S(1)} all-to-all(f32[2,8,2048]{2,1,0:T(8,128)S(1)} %broadcast_in_dim.6), channel_id=1, replica_groups=mesh['pair'=2,'dp_0'=4,'dp_1'=8,'ep'=8] {'pair'}, dimensions={0} | all-to-all | bytes 262144 | tf_op jit(solution)/shard_map/all_to_all | solution.py:18
  131.3 2.5 %broadcast_in_dim.7 = f32[32,2,8,2048]{3,2,1,0:T(8,128)} broadcast(f32[2,8,2048]{2,1,0:T(8,128)S(1)} %all_to_all.22), dimensions={1,2,3} | broadcast | bytes 4325376 | tf_op jit(solution)/shard_map/broadcast_in_dim | solution.py:17
  133.8 4.8 %all-to-all-start.3 = ((f32[32,2,8,2048]{3,2,1,0:T(8,128)}), f32[32,2,8,2048]{3,2,1,0:T(8,128)}, u32[]{:S(2)}, u32[]{:S(2)}) async-start(f32[32,2,8,2048]{3,2,1,0:T(8,128)} %broadcast_in_dim.7), calls=%async_computation.3 | async-start | bytes 8388608 | tf_op jit(solution)/shard_map/all_to_all | solution.py:18
  138.6 93.9 %all-to-all-done.3 = f32[32,2,8,2048]{3,2,1,0:T(8,128)} async-done(((f32[32,2,8,2048]{3,2,1,0:T(8,128)}), f32[32,2,8,2048]{3,2,1,0:T(8,128)}, u32[]{:S(2)}, u32[]{:S(2)}) %all-to-all-start.3) | async-done | bytes 4194336 | tf_op jit(solution)/shard_map/all_to_all | solution.py:18
  232.5 2.5 %copy.7 = f32[32,2,8,2048]{3,2,0,1:T(8,128)S(1)} copy(f32[32,2,8,2048]{3,2,1,0:T(8,128)} %all-to-all-done.3) | data formatting | bytes 8388608 | tf_op jit(solution)/shard_map/all_to_all | solution.py:18
  235.0 1.1 multiply_convert_fusion
  (2 shorter events, 0.0 us)
Async XLA Ops:
  0.0 1.9 copy-start
  133.8 98.7 %all-to-all-start.3 = ((f32[32,2,8,2048]{3,2,1,0:T(8,128)}), f32[32,2,8,2048]{3,2,1,0:T(8,128)}, u32[]{:S(2)}, u32[]{:S(2)}) async-start(f32[32,2,8,2048]{3,2,1,0:T(8,128)} %broadcast_in_dim.7), calls=%async_computation.3 | async-start | bytes 8388608 | tf_op jit(solution)/shard_map/all_to_all | solution.py:18
where the time goes:
time: 237 us; the launch traced here: 236 us
  blocking collectives  124 us (52%)
  waiting for transfers between devices  93.9 us (40%)
  local copies, waits for them, and re-layouts  7.32 us (3%)
  starting transfers between devices  4.85 us (2%)
  other arithmetic  3.55 us (1%)
  matrix products  2.96 us (1%)
    all_to_all x1, blocking collectives, summed_on_arrival(): parts = lax.all_to_all(split_up(x, dim, peers), axis, 0, 0, tiled=True)  109 us
    all_to_all x1, waiting for transfers between devices, copy_for_each(): return lax.all_to_all(copies, axis, split_axis=0, concat_axis=0, tiled=True)  93.9 us
    all_to_all x1, blocking collectives, sum_by_axis(): lax.all_to_all(nearer, far, split_axis=0, concat_axis=0, tiled=True)  7.47 us
    all_to_all x1, blocking collectives, copy_for_each(): return lax.all_to_all(copies, axis, split_axis=0, concat_axis=0, tiled=True)  6.85 us
    all_to_all x1, starting transfers between devices, copy_for_each(): return lax.all_to_all(copies, axis, split_axis=0, concat_axis=0, tiled=True)  4.85 us
  transfers between devices with their start and end apart: 1, of which 1 were waited for; matrix products, arithmetic and copies ran while one was open for 0% of the time, Pallas kernels for 0%

commit v1 on v0

v1 whole, which is shorter than its diff:
```python
import heapq

import jax
import jax.numpy as jnp
from jax import lax
from jax.experimental import pallas as pl
from jax.experimental.pallas import tpu as pltpu
from jax.sharding import Mesh
from jax.sharding import PartitionSpec as P

SIZE = {"pair": 2, "x": 4, "z": 8}
MESH = pl.DeviceIdType.MESH
ROWS = 16
ORDERS = (("x", "z", "pair"), ("z", "x", "pair"), ("x", "z", "pair"), ("z", "x", "pair"))
BYTES_PER_US = 46600.0
HOP_US, FURTHER_US, TASK_US = 1.9, 0.75, 0.1


def wrapped(index, n):
    return lax.rem(index + n, n)


class Flow:
    def __init__(self, send_sems, recv_sems):
        self.send_sems, self.recv_sems = send_sems, recv_sems
        self.now, self.free, self.heap, self.copies = 0.0, {}, [], []

    def send(self, axis, delta, src, dst, then):
        n = SIZE[axis]
        k = len(self.copies)
        peer = wrapped(lax.axis_index(axis) + delta, n)
        copy = pltpu.make_async_remote_copy(
            src_ref=src,
            dst_ref=dst,
            send_sem=self.send_sems.at[k],
            recv_sem=self.recv_sems.at[k],
            device_id={axis: peer},
            device_id_type=MESH,
        )
        copy.start()
        hops = abs(delta)
        size = 1
        for d in dst.shape:
            size *= d
        size *= jnp.dtype(dst.dtype).itemsize
        link = (axis, delta > 0)
        begin = max(self.now, self.free.get(link, 0.0))
        end = begin + hops * size / BYTES_PER_US
        self.free[link] = end
        heapq.heappush(self.heap, (end + HOP_US + FURTHER_US * (hops - 1), k, then))
        self.copies.append(copy)

    def run(self):
        while self.heap:
            at, k, then = heapq.heappop(self.heap)
            self.now = max(self.now, at) + TASK_US
            self.copies[k].wait_recv()
            then()
        for copy in self.copies:
            copy.wait_send()


def add_into(dst, src):
    if len(dst.shape) > 3:
        for i in range(dst.shape[0]):
            add_into(dst.at[i], src.at[i])
    else:
        dst[...] += src[...]


def reduce_stage(flow, axis, part, slots, done):
    n = SIZE[axis]
    me = lax.axis_index(axis)
    if n == 2:
        mine = part.at[me]

        def last():
            add_into(mine, slots[0].at[0])
            done(mine)

        flow.send(axis, 1, part.at[1 - me], slots[0].at[0], last)
        return
    steps = n // 2
    middle = part.shape[1] // 2
    left = [2]

    def advance(sign, step):
        slot = slots[0 if sign > 0 else 1]
        if step == 0:
            half = pl.ds(0, middle) if sign > 0 else pl.ds(middle, middle)
            chunk = part.at[wrapped(me + sign * steps, n), half]
            target = slot.at[0, pl.ds(0, middle)]
        else:
            chunk = part.at[wrapped(me + sign * (steps - step), n)]
            target = slot.at[step]

        def arrived():
            nearer = part.at[wrapped(me + sign * (steps - step - 1), n)]
            if step == 0:
                half = pl.ds(0, middle) if sign > 0 else pl.ds(middle, middle)
                add_into(nearer.at[half], target)
            else:
                add_into(nearer, target)
            if step + 1 < steps:
                advance(sign, step + 1)
                return
            left[0] -= 1
            if left[0] == 0:
                done(part.at[me])

        flow.send(axis, sign * 1, chunk, target, arrived)

    advance(1, 0)
    advance(-1, 0)


def block_of(out, at):
    everything = slice(None)
    return out.at[at.get("x", everything), at.get("z", everything)]


def gather_direct(flow, axis, out, at, done):
    n = SIZE[axis]
    me = lax.axis_index(axis)
    left = [n - 1]

    def arrived():
        left[0] -= 1
        if left[0] == 0:
            done()

    mine = block_of(out, at)
    for far in range(1, n // 2 + 1):
        for delta in (far, -far) if 2 * far < n else (far,):
            flow.send(axis, delta, mine, mine, arrived)


def gather_ring(flow, axis, out, at, done):
    n = SIZE[axis]
    me = lax.axis_index(axis)
    steps = n // 2
    left = [2]

    def advance(sign, step):
        block = block_of(out, {**at, axis: wrapped(me - sign * step, n)})
        if step == steps - 1:
            half = block.shape[0] // 2
            block = block.at[pl.ds(0 if sign > 0 else half, half)]

        def arrived():
            if step + 1 < steps:
                advance(sign, step + 1)
                return
            left[0] -= 1
            if left[0] == 0:
                done()

        flow.send(axis, sign, block, block, arrived)

    advance(1, 0)
    advance(-1, 0)


def kernel(replicas, a_ref, b_ref, out_ref, at_ref, *refs):
    n_inst = len(ORDERS)
    parts = refs[:n_inst]
    refs = refs[n_inst:]
    slots = []
    for order in ORDERS:
        own = []
        for axis in order:
            take = 1 if SIZE[axis] == 2 else 2
            own.append(refs[:take])
            refs = refs[take:]
        slots.append(own)
    send_sems, recv_sems = refs

    barrier = pltpu.get_barrier_semaphore()
    peers = 0
    for axis, n in SIZE.items():
        for delta in range(1, n):
            peer = wrapped(lax.axis_index(axis) + delta, n)
            pl.semaphore_signal(barrier, inc=1, device_id={axis: peer}, device_id_type=MESH)
            peers += 1

    at_ref[...] = a_ref[...].T
    for z in range(SIZE["z"]):
        total = jnp.dot(at_ref[...], b_ref[:, z * 256 : (z + 1) * 256], preferred_element_type=jnp.float32)
        for half in range(2):
            for x in range(SIZE["x"]):
                for i, order in enumerate(ORDERS):
                    first = half * 256 + x * 64 + i * ROWS
                    index = {"pair": half, "x": x, "z": z}
                    parts[i][tuple(index[axis] for axis in order)] = total[first : first + ROWS]

    pl.semaphore_wait(barrier, peers)
    flow = Flow(send_sems, recv_sems)

    def start(i):
        order = ORDERS[i]
        out = out_ref.at[i]
        here = {axis: lax.axis_index(axis) for axis in ("x", "z")}

        def gathered():
            pass

        def second_gather():
            gather_ring(flow, order[0], out, {}, gathered)

        def finish(piece):
            out[here["x"], here["z"]] = (piece[...] / replicas).astype(jnp.bfloat16)
            gather_direct(flow, order[1], out, dict(here), second_gather)

        def stage(k, part):
            if k == len(order):
                finish(part)
                return
            reduce_stage(flow, order[k], part, slots[i][k], lambda chunk: stage(k + 1, chunk))

        stage(0, parts[i])

    for i in range(n_inst):
        start(i)
    flow.run()


def local(activations, cotangents):
    rows, columns = activations.shape[1], cotangents.shape[1]
    piece = (ROWS, columns // SIZE["z"])
    replicas = SIZE["pair"] * SIZE["x"] * SIZE["z"]
    scratch = [pltpu.VMEM((rows, activations.shape[0]), jnp.bfloat16)]
    for order in ORDERS:
        scratch.append(pltpu.VMEM(tuple(SIZE[a] for a in order) + piece, jnp.float32))
    copies = 0
    for order in ORDERS:
        for k, axis in enumerate(order):
            chunk = tuple(SIZE[a] for a in order[k + 1 :]) + piece
            steps = SIZE[axis] // 2
            take = 1 if SIZE[axis] == 2 else 2
            scratch += [pltpu.VMEM((steps,) + chunk, jnp.float32)] * take
            copies += take * steps
        copies += SIZE[order[1]] - 1 + SIZE[order[0]]
    scratch += [pltpu.SemaphoreType.DMA((copies,))] * 2
    out = pl.pallas_call(
        lambda *refs: kernel(replicas, *refs),
        out_shape=jax.ShapeDtypeStruct((len(ORDERS), SIZE["x"], SIZE["z"]) + piece, jnp.bfloat16),
        in_specs=[pl.BlockSpec(memory_space=pltpu.VMEM)] * 2,
        out_specs=pl.BlockSpec(memory_space=pltpu.VMEM),
        scratch_shapes=scratch,
        compiler_params=pltpu.CompilerParams(collective_id=0, has_side_effects=True),
        name="grad_sum",
    )(activations, cotangents)
    return out.transpose(1, 0, 3, 2, 4).reshape(rows // SIZE["pair"], columns)


def solution(mesh):
    split = Mesh(
        mesh.devices.reshape(mesh.shape["pair"], SIZE["x"], SIZE["z"], mesh.shape["ep"]),
        ("pair", "x", "z", "ep"),
    )
    placed = P(("pair", "x", "z"), "ep")
    return jax.shard_map(
        local, mesh=split, in_specs=(placed, placed), out_specs=P("pair", "ep"), check_vma=False
    )
```

time: 237 us -> 75.1 us (0.32)
  the two profiles are of different devices: /device:TPU:32 before, /device:TPU:16 now
where the time goes in v1:
time: 75.1 us; the launch traced here: 74.9 us
  Pallas kernels  72 us (96%)
  local copies, waits for them, and re-layouts  2.93 us (4%)
    pallas_call x1, Pallas kernels, local(): pl.pallas_call(lambda *refs: kernel(replicas, *refs), out_shape=jax.Shape...  72 us
    transpose x1, local copies, waits for them, and re-layouts, local(): return out.transpose(1, 0, 3, 2, 4).reshape(rows // SIZE['pair'], columns)  1.65 us

profile of v1, /device:TPU:16, one launch (start us, length us, event | category | flops | bytes accessed | tf_op | source)
XLA Modules:
  0.0 74.9 jit_solution(18430594108699645333)
XLA Ops:
  0.0 72.0 %grad_sum.1 = bf16[4,4,8,16,256]{4,3,2,1,0:T(8,128)(2,1)} custom-call(bf16[768,512]{1,0:T(8,128)(2,1)} %refs_0_.1, bf16[768,2048]{1,0:T(8,128)(2,1)} %refs_1_.1), custom_call_target="tpu_custom_call" | custom-call | tf_op jit(solution)/shard_map/grad_sum/pallas_call | solution.py:244
  72.0 1.6 %copy.3 = bf16[4,4,16,8,256]{4,3,2,1,0:T(8,128)(2,1)S(1)} copy(bf16[4,4,16,8,256]{4,2,3,0,1:T(8,128)(2,1)} %bitcast.4) | data formatting | bytes 2097152 | tf_op jit(solution)/shard_map/transpose | solution.py:253
  73.6 1.3 %copy.4 = bf16[32,8,8,256]{3,1,2,0:T(8,128)(2,1)} copy(bf16[32,8,8,256]{3,2,1,0:T(8,128)(2,1)S(1)} %bitcast.5) | data formatting | bytes 2097152

commit v2 on v0

v2 whole, which is shorter than its diff:
```python
import heapq
import math

import jax
import jax.numpy as jnp
from jax import lax
from jax.experimental import pallas as pl
from jax.experimental.pallas import tpu as pltpu
from jax.sharding import Mesh
from jax.sharding import PartitionSpec as P

SIZE = {"pair": 2, "x": 4, "z": 8}
MESH = pl.DeviceIdType.MESH
LEAF = (16, 128)
STRIPS = 4
SIDES = 2
X_STRIPS = (2, 2)
X_FIRST = ((("ring", "x"), ("ring", "pair"), ("direct", "z")), (("direct", "z"), ("ring", "x")))
Z_FIRST = ((("ring", "z"), ("ring", "pair"), ("direct", "x")), (("direct", "z"), ("ring", "x")))
RULER = 256
BYTES_PER_US = 46600.0
HOP_US, FURTHER_US, TASK_US = 2.65, 0.9, 0.03


def units():
    found = []
    for k in range(STRIPS):
        for side in range(SIDES):
            split = X_STRIPS[side]
            if k < split:
                found.append((k, side, X_FIRST))
            if STRIPS - 1 - k >= split:
                found.append((STRIPS - 1 - k, side, Z_FIRST))
    return found


def order_of(plan):
    return tuple(axis for _, axis in plan[0])


def wrapped(index, n):
    return lax.rem(index + n, n)


class Flow:
    def __init__(self, send_sems, recv_sems, ruler):
        self.send_sems, self.recv_sems, self.ruler = send_sems, recv_sems, ruler
        self.now, self.free, self.heap, self.waits = 0.0, {}, [], 0
        self.sent = {}

    def send(self, unit, axis, copies, arriving, then):
        k = self.waits
        self.waits += 1
        latest = 0.0
        for delta, src, dst in copies:
            pltpu.make_async_remote_copy(
                src_ref=src,
                dst_ref=dst,
                send_sem=self.send_sems.at[unit],
                recv_sem=self.recv_sems.at[k],
                device_id={axis: wrapped(lax.axis_index(axis) + delta, SIZE[axis])},
                device_id_type=MESH,
            ).start()
            hops = abs(delta)
            size = math.prod(dst.shape) * jnp.dtype(dst.dtype).itemsize
            self.sent[unit] = self.sent.get(unit, 0) + size
            link = (axis, delta > 0)
            end = max(self.now, self.free.get(link, 0.0)) + hops * size / BYTES_PER_US
            self.free[link] = end
            latest = max(latest, end + HOP_US + FURTHER_US * (hops - 1))
        heapq.heappush(self.heap, (latest, k, arriving, then))

    def run(self):
        while self.heap:
            at, k, arriving, then = heapq.heappop(self.heap)
            self.now = max(self.now, at) + TASK_US
            pltpu.make_async_copy(arriving, arriving, self.recv_sems.at[k]).wait()
            then()
        for unit, size in self.sent.items():
            row = math.prod(self.ruler.shape[1:]) * jnp.dtype(self.ruler.dtype).itemsize
            assert size % row == 0 and size // row <= self.ruler.shape[0]
            total = self.ruler.at[pl.ds(0, size // row)]
            pltpu.make_async_copy(total, total, self.send_sems.at[unit]).wait()


def add_into(dst, *sources):
    if len(dst.shape) > 3:
        for i in range(dst.shape[0]):
            add_into(dst.at[i], *(source.at[i] for source in sources))
    else:
        total = dst[...]
        for source in sources:
            total += source[...]
        dst[...] = total


def slots_of(kind, axis):
    n = SIZE[axis]
    return n - 1 if kind == "direct" or n == 2 else 2 * (n // 2)


def waits_of(kind, axis):
    return 1 if kind == "direct" else slots_of(kind, axis)


def deltas_of(n):
    return [d for far in range(1, n // 2 + 1) for d in ((far, -far) if 2 * far < n else (far,))]


def reduce_direct(flow, unit, axis, part, slots, done):
    n = SIZE[axis]
    me = lax.axis_index(axis)

    def arrived():
        add_into(part.at[me], *(slots.at[i] for i in range(n - 1)))
        done(part.at[me])

    copies = [(delta, part.at[wrapped(me + delta, n)], slots.at[i]) for i, delta in enumerate(deltas_of(n))]
    flow.send(unit, axis, copies, slots, arrived)


def reduce_ring(flow, unit, axis, part, slots, done):
    n = SIZE[axis]
    me = lax.axis_index(axis)
    steps = n // 2
    middle = part.shape[1] // 2
    left = [2]

    def advance(sign, step):
        slot = slots.at[step if sign > 0 else steps + step]
        chunk = part.at[wrapped(me + sign * (steps - step), n)]
        nearer = part.at[wrapped(me + sign * (steps - step - 1), n)]
        if step == 0:
            half = pl.ds(0 if sign > 0 else middle, middle)
            slot, chunk, nearer = slot.at[pl.ds(0, middle)], chunk.at[half], nearer.at[half]

        def arrived():
            add_into(nearer, slot)
            if step + 1 < steps:
                advance(sign, step + 1)
                return
            left[0] -= 1
            if left[0] == 0:
                done(part.at[me])

        flow.send(unit, axis, [(sign, chunk, slot)], slot, arrived)

    advance(1, 0)
    advance(-1, 0)


def gather_direct(flow, unit, axis, block_at, at, done):
    mine = block_at({**at, axis: lax.axis_index(axis)})
    deltas = deltas_of(SIZE[axis])
    flow.send(unit, axis, [(delta, mine, mine) for delta in deltas], block_at(at, 0, len(deltas)), done)


def gather_ring(flow, unit, axis, block_at, at, done):
    n = SIZE[axis]
    me = lax.axis_index(axis)
    steps = n // 2
    left = [2]

    def advance(sign, step):
        place = {**at, axis: wrapped(me - sign * step, n)}
        block = block_at(place, sign if step == steps - 1 else 0)

        def arrived():
            if step + 1 < steps:
                advance(sign, step + 1)
                return
            left[0] -= 1
            if left[0] == 0:
                done()

        flow.send(unit, axis, [(sign, block, block)], block, arrived)

    advance(1, 0)
    advance(-1, 0)


REDUCE = {"ring": reduce_ring, "direct": reduce_direct}
GATHER = {"ring": gather_ring, "direct": gather_direct}


def start_unit(flow, number, unit, part, slots, out, replicas):
    strip, side, (reduce_plan, gather_plan) = unit
    height, width = LEAF
    extent = SIZE["z"] * width

    def block_at(at, half=0, count=None):
        x = at.get("x", pl.ds(0, count or SIZE["x"]))
        cols = pl.ds(side * extent, count * width if count else extent)
        if "z" in at:
            cols = pl.ds(pl.multiple_of(side * extent + at["z"] * width, width), width)
        if half and "z" in at:
            x = pl.ds(0 if half > 0 else SIZE["x"] // 2, SIZE["x"] // 2)
        elif half:
            cols = pl.ds(side * extent + (0 if half > 0 else extent // 2), extent // 2)
        return out.at[x, strip, :, cols]

    def gather(k):
        if k < len(gather_plan):
            kind, axis = gather_plan[k]
            rest = {other: lax.axis_index(other) for _, other in gather_plan[k + 1 :]}
            GATHER[kind](flow, number, axis, block_at, rest, lambda: gather(k + 1))

    def reduce(k, chunk):
        if k < len(reduce_plan):
            kind, axis = reduce_plan[k]
            if SIZE[axis] == 2:
                kind = "direct"
            REDUCE[kind](flow, number, axis, chunk, slots[k], lambda mine: reduce(k + 1, mine))
            return
        own = block_at({axis: lax.axis_index(axis) for axis in ("x", "z")})
        own[...] = (chunk[...] / replicas).astype(jnp.bfloat16)
        gather(0)

    reduce(0, part)


def kernel(replicas, a_hbm, b_hbm, out, a_ref, b_ref, for_x, for_z, ruler, in_sems, send_sems, recv_sems, *refs):
    work = units()
    parts, refs = refs[: len(work)], list(refs[len(work) :])
    slots = [[refs.pop(0) for _ in unit[2][0]] for unit in work]
    height, width = LEAF
    rows, tokens = for_x.shape
    extent = SIZE["z"] * width

    cuts = in_sems.shape[0] - 1
    load_a = pltpu.make_async_copy(a_hbm, a_ref, in_sems.at[cuts])
    load_a.start()
    loads_b = []
    for i in range(cuts):
        cut = pl.ds(i * (tokens // cuts), tokens // cuts)
        loads_b.append(pltpu.make_async_copy(b_hbm.at[cut], b_ref.at[cut], in_sems.at[i]))
        loads_b[-1].start()

    barrier = pltpu.get_barrier_semaphore()
    peers = 0
    for axis, n in SIZE.items():
        for delta in range(1, n):
            peer = wrapped(lax.axis_index(axis) + delta, n)
            pl.semaphore_signal(barrier, inc=1, device_id={axis: peer}, device_id_type=MESH)
            peers += 1

    group = 2 * height
    load_a.wait()
    for first in range(0, rows, 128):
        turned = a_ref[:, first : first + 128].T
        for row in range(first, first + 128, height):
            half, rest = divmod(row, rows // 2)
            x, rest = divmod(rest, rows // 2 // SIZE["x"])
            strip = rest // height
            piece = turned[row - first : row - first + height]
            for_x[pl.ds((x * STRIPS + strip) * group + half * height, height), :] = piece
            for_z[pl.ds((strip * SIZE["x"] + x) * group + half * height, height), :] = piece
    for load in loads_b:
        load.wait()

    def part_of(strip, side):
        for unit, part in zip(work, parts):
            if unit[:2] == (strip, side):
                return part

    def multiply_x(x):
        for side in range(SIDES):
            strips = X_STRIPS[side]
            if strips == 0:
                continue
            left = for_x[pl.ds(pl.multiple_of(x * (STRIPS * group), group), strips * group), :]
            for z in range(0, SIZE["z"], 2):
                column = side * extent + z * width
                total = jnp.dot(left, b_ref[:, column : column + 2 * width], preferred_element_type=jnp.float32)
                for strip in range(strips):
                    for half in range(2):
                        top = strip * group + half * height
                        for k in range(2):
                            part_of(strip, side)[x, half, z + k] = total[top : top + height, k * width : (k + 1) * width]

    def multiply_z(z):
        for side in range(SIDES):
            split = X_STRIPS[side]
            if split == STRIPS:
                continue
            left = for_z[split * SIZE["x"] * group :, :]
            column = pl.multiple_of(side * extent + z * width, width)
            total = jnp.dot(left, b_ref[:, pl.ds(column, width)], preferred_element_type=jnp.float32)
            for strip in range(split, STRIPS):
                for x in range(SIZE["x"]):
                    for half in range(2):
                        top = ((strip - split) * SIZE["x"] + x) * group + half * height
                        part_of(strip, side)[z, half, x] = total[top : top + height]

    me = {axis: lax.axis_index(axis) for axis in SIZE}
    flow = Flow(send_sems, recv_sems, ruler)
    multiply_z(wrapped(me["z"] + SIZE["z"] // 2, SIZE["z"]))
    multiply_x(wrapped(me["x"] + SIZE["x"] // 2, SIZE["x"]))
    pl.semaphore_wait(barrier, peers)
    for number, unit in enumerate(work):
        start_unit(flow, number, unit, parts[number], slots[number], out, replicas)
    for far in range(SIZE["z"] // 2 - 1, 0, -1):
        if far < SIZE["x"] // 2:
            multiply_x(wrapped(me["x"] + far, SIZE["x"]))
            multiply_x(wrapped(me["x"] - far, SIZE["x"]))
        multiply_z(wrapped(me["z"] + far, SIZE["z"]))
        multiply_z(wrapped(me["z"] - far, SIZE["z"]))
    multiply_x(me["x"])
    multiply_z(me["z"])
    flow.run()


def local(activations, cotangents):
    tokens, rows = activations.shape
    columns = cotangents.shape[1]
    work = units()
    scratch = [
        pltpu.VMEM((tokens, rows), jnp.bfloat16),
        pltpu.VMEM((tokens, columns), jnp.bfloat16),
        pltpu.VMEM((rows, tokens), jnp.bfloat16),
        pltpu.VMEM((rows, tokens), jnp.bfloat16),
        pltpu.VMEM((RULER,) + LEAF, jnp.bfloat16),
        pltpu.SemaphoreType.DMA((5,)),
    ]
    parts, slots, waits = [], [], 0
    for _, _, plan in work:
        order = order_of(plan)
        parts.append(pltpu.VMEM(tuple(SIZE[axis] for axis in order) + LEAF, jnp.float32))
        for k, (kind, axis) in enumerate(plan[0]):
            chunk = tuple(SIZE[other] for other in order[k + 1 :]) + LEAF
            slots.append(pltpu.VMEM((slots_of(kind, axis),) + chunk, jnp.float32))
        waits += sum(waits_of(kind, axis) for stages in plan for kind, axis in stages)
    scratch += [pltpu.SemaphoreType.DMA((len(work),)), pltpu.SemaphoreType.DMA((waits,))] + parts + slots
    replicas = math.prod(SIZE.values())
    shape = (SIZE["x"], STRIPS, LEAF[0], columns)
    out = pl.pallas_call(
        lambda *refs: kernel(replicas, *refs),
        out_shape=pltpu.VMEM(shape, jnp.bfloat16),
        in_specs=[pl.BlockSpec(memory_space=pl.ANY)] * 2,
        out_specs=pl.BlockSpec(memory_space=pltpu.VMEM),
        scratch_shapes=scratch,
        compiler_params=pltpu.CompilerParams(collective_id=0, has_side_effects=True),
        name="grad_sum",
    )(activations, cotangents)
    return out.reshape(rows // SIZE["pair"], columns)


def solution(mesh):
    split = Mesh(
        mesh.devices.reshape(mesh.shape["pair"], SIZE["x"], SIZE["z"], mesh.shape["ep"]),
        ("pair", "x", "z", "ep"),
    )
    placed = P(("pair", "x", "z"), "ep")
    return jax.shard_map(
        local, mesh=split, in_specs=(placed, placed), out_specs=P("pair", "ep"), check_vma=False
    )
```

time: 237 us -> 59.7 us (0.25)
  the two profiles are of different devices: /device:TPU:32 before, /device:TPU:16 now
where the time goes in v2:
time: 59.7 us; the launch traced here: 59.6 us
  Pallas kernels  58.6 us (98%)
  local copies, waits for them, and re-layouts  0.97 us (2%)
    pallas_call x1, Pallas kernels, local(): pl.pallas_call(lambda *refs: kernel(replicas, *refs), out_shape=pltpu.VME...  58.6 us

profile of v2, /device:TPU:16, one launch (start us, length us, event | category | flops | bytes accessed | tf_op | source)
XLA Modules:
  0.0 59.6 jit_solution(10185641393612468610)
XLA Ops:
  0.0 58.6 %grad_sum.1 = bf16[4,4,16,2048]{3,2,1,0:T(8,128)(2,1)S(1)} custom-call(bf16[768,512]{1,0:T(8,128)(2,1)} %refs_0_.1, bf16[768,2048]{1,0:T(8,128)(2,1)} %refs_1_.1), custom_call_target="tpu_custom_call" | custom-call | tf_op jit(solution)/shard_map/grad_sum/pallas_call | solution.py:336
  58.6 1.0 %copy.4 = bf16[256,2048]{1,0:T(8,128)(2,1)} copy(bf16[256,2048]{1,0:T(8,128)(2,1)S(1)} %bitcast.1) | data formatting | bytes 2097152

commit v3 on v2

--- a/solution.py
+++ b/solution.py
@@ -15,11 +15,13 @@
 STRIPS = 4
 SIDES = 2
 X_STRIPS = (2, 2)
-X_FIRST = ((("ring", "x"), ("ring", "pair"), ("direct", "z")), (("direct", "z"), ("ring", "x")))
-Z_FIRST = ((("ring", "z"), ("ring", "pair"), ("direct", "x")), (("direct", "z"), ("ring", "x")))
-RULER = 256
+X_FIRST = ((("coded", "x"), ("ring", "pair"), ("direct", "z")), (("direct", "z"), ("ring", "x")))
+Z_FIRST = ((("coded", "z"), ("ring", "pair"), ("direct", "x")), (("direct", "z"), ("ring", "x")))
+GROUP = 4
+CODE_POWER, CODE_STEEP, CODE_LOW = 36, 120.0, 2.0**-3.45
+RULER = 320
 BYTES_PER_US = 46600.0
-HOP_US, FURTHER_US, TASK_US = 2.65, 0.9, 0.03
+HOP_US, FURTHER_US, TASK_US = 2.65, 0.9, 0.15
 
 
 def units():
@@ -179,7 +181,97 @@
     advance(-1, 0)
 
 
-REDUCE = {"ring": reduce_ring, "direct": reduce_direct}
+def magnitudes(x):
+    return jnp.max(jnp.abs(x), axis=0)
+
+
+def encode(x, scale):
+    y = jnp.abs(x) * (CODE_STEEP * CODE_LOW / jnp.maximum(scale, 1e-35)) + CODE_LOW
+    y4 = y * y * (y * y)
+    y8 = y4 * y4
+    y16 = y8 * y8
+    y = y16 * y16 * y4
+    return jnp.where(x < 0, -y, y).astype(jnp.bfloat16)
+
+
+def decode(code, scale):
+    y = code.astype(jnp.float32)
+    root = jnp.exp(jnp.log(jnp.abs(y)) * (1 / CODE_POWER) - math.log(CODE_LOW))
+    x = (root - 1) * (scale * (1 / CODE_STEEP))
+    return jnp.where(y < 0, -x, x)
+
+
+def coded_rows(shape):
+    return math.prod(shape[:-1]) + 8
+
+
+def groups_of(chunk):
+    if len(chunk.shape) == 3:
+        return [chunk.at[pl.ds(i, GROUP)] for i in range(0, chunk.shape[0], GROUP)]
+    return [group for i in range(chunk.shape[0]) for group in groups_of(chunk.at[i])]
+
+
+def group_rows(k):
+    rows = GROUP * LEAF[0]
+    return pl.ds(8 + k * rows, rows)
+
+
+def write_code(chunk, wire):
+    shape = (GROUP * LEAF[0] // 8, 8, LEAF[1])
+    groups = groups_of(chunk)
+    scale = magnitudes(groups[0][...].reshape(shape))
+    for group in groups[1:]:
+        scale = jnp.maximum(scale, magnitudes(group[...].reshape(shape)))
+    scale = scale.astype(jnp.bfloat16)
+    wire[pl.ds(0, 8), :] = scale
+    scale = scale.astype(jnp.float32)
+    for k, group in enumerate(groups):
+        wire[group_rows(k), :] = encode(group[...].reshape(shape), scale).reshape(-1, LEAF[1])
+
+
+def add_code(chunk, wire):
+    shape = (GROUP * LEAF[0] // 8, 8, LEAF[1])
+    scale = wire[pl.ds(0, 8), :].astype(jnp.float32)
+    for k, group in enumerate(groups_of(chunk)):
+        value = decode(wire[group_rows(k), :].reshape(shape), scale)
+        group[...] += value.reshape(group.shape)
+
+
+def reduce_coded(flow, unit, axis, part, slots, done):
+    wires_in, wires_out = slots
+    n = SIZE[axis]
+    me = lax.axis_index(axis)
+    steps = n // 2
+    middle = part.shape[1] // 2
+    left = [2]
+
+    def advance(sign, step):
+        index = step if sign > 0 else steps + step
+        chunk = part.at[wrapped(me + sign * (steps - step), n)]
+        nearer = part.at[wrapped(me + sign * (steps - step - 1), n)]
+        if step == 0:
+            half = pl.ds(0 if sign > 0 else middle, middle)
+            chunk, nearer = chunk.at[half], nearer.at[half]
+        rows = pl.ds(0, coded_rows(chunk.shape))
+        source, target = wires_out.at[index, rows], wires_in.at[index, rows]
+
+        def arrived():
+            add_code(nearer, target)
+            if step + 1 < steps:
+                advance(sign, step + 1)
+                return
+            left[0] -= 1
+            if left[0] == 0:
+                done(part.at[me])
+
+        write_code(chunk, source)
+        flow.send(unit, axis, [(sign, source, target)], target, arrived)
+
+    advance(1, 0)
+    advance(-1, 0)
+
+
+REDUCE = {"ring": reduce_ring, "direct": reduce_direct, "coded": reduce_coded}
 GATHER = {"ring": gather_ring, "direct": gather_direct}
 
 
@@ -222,7 +314,9 @@
 def kernel(replicas, a_hbm, b_hbm, out, a_ref, b_ref, for_x, for_z, ruler, in_sems, send_sems, recv_sems, *refs):
     work = units()
     parts, refs = refs[: len(work)], list(refs[len(work) :])
-    slots = [[refs.pop(0) for _ in unit[2][0]] for unit in work]
+    slots = []
+    for _, _, plan in work:
+        slots.append([(refs.pop(0), refs.pop(0)) if kind == "coded" else refs.pop(0) for kind, _ in plan[0]])
     height, width = LEAF
     rows, tokens = for_x.shape
     extent = SIZE["z"] * width
@@ -319,7 +413,7 @@
         pltpu.VMEM((tokens, columns), jnp.bfloat16),
         pltpu.VMEM((rows, tokens), jnp.bfloat16),
         pltpu.VMEM((rows, tokens), jnp.bfloat16),
-        pltpu.VMEM((RULER,) + LEAF, jnp.bfloat16),
+        pltpu.VMEM((RULER, 8, LEAF[1]), jnp.bfloat16),
         pltpu.SemaphoreType.DMA((5,)),
     ]
     parts, slots, waits = [], [], 0
@@ -328,7 +422,10 @@
         parts.append(pltpu.VMEM(tuple(SIZE[axis] for axis in order) + LEAF, jnp.float32))
         for k, (kind, axis) in enumerate(plan[0]):
             chunk = tuple(SIZE[other] for other in order[k + 1 :]) + LEAF
-            slots.append(pltpu.VMEM((slots_of(kind, axis),) + chunk, jnp.float32))
+            if kind == "coded":
+                slots += [pltpu.VMEM((slots_of(kind, axis), coded_rows(chunk), LEAF[1]), jnp.bfloat16)] * 2
+            else:
+                slots.append(pltpu.VMEM((slots_of(kind, axis),) + chunk, jnp.float32))
         waits += sum(waits_of(kind, axis) for stages in plan for kind, axis in stages)
     scratch += [pltpu.SemaphoreType.DMA((len(work),)), pltpu.SemaphoreType.DMA((waits,))] + parts + slots
     replicas = math.prod(SIZE.values())

time: 59.7 us -> 53.4 us (0.89)
  Pallas kernels: 58.6 us -> 52.3 us
    pallas_call x1, Pallas kernels: 58.6 us -> 52.3 us  [local(): pl.pallas_call(lambda *refs: kernel(replicas, *refs), out_shape=pltpu.VME...]
where the time goes in v3:
time: 53.4 us; the launch traced here: 53.3 us
  Pallas kernels  52.3 us (98%)
  local copies, waits for them, and re-layouts  0.97 us (2%)
    pallas_call x1, Pallas kernels, local(): pl.pallas_call(lambda *refs: kernel(replicas, *refs), out_shape=pltpu.VME...  52.3 us

profile of v3, /device:TPU:16, one launch (start us, length us, event | category | flops | bytes accessed | tf_op | source)
XLA Modules:
  0.0 53.3 jit_solution(8123175360535994908)
XLA Ops:
  0.0 52.3 %grad_sum.1 = bf16[4,4,16,2048]{3,2,1,0:T(8,128)(2,1)S(1)} custom-call(bf16[768,512]{1,0:T(8,128)(2,1)} %refs_0_.1, bf16[768,2048]{1,0:T(8,128)(2,1)} %refs_1_.1), custom_call_target="tpu_custom_call" | custom-call | tf_op jit(solution)/shard_map/grad_sum/pallas_call | solution.py:433
  52.4 1.0 %copy.4 = bf16[256,2048]{1,0:T(8,128)(2,1)} copy(bf16[256,2048]{1,0:T(8,128)(2,1)S(1)} %bitcast.1) | data formatting | bytes 2097152

commit v4 on v3

--- a/solution.py
+++ b/solution.py
@@ -14,9 +14,13 @@
 LEAF = (16, 128)
 STRIPS = 4
 SIDES = 2
-X_STRIPS = (2, 2)
-X_FIRST = ((("coded", "x"), ("ring", "pair"), ("direct", "z")), (("direct", "z"), ("ring", "x")))
-Z_FIRST = ((("coded", "z"), ("ring", "pair"), ("direct", "x")), (("direct", "z"), ("ring", "x")))
+X_STRIPS = (3, 2)
+X_FIRST = (("coded", "x"), ("direct", "pair"), ("direct", "z"))
+Z_FIRST = (("coded", "z"), ("direct", "pair"), ("direct", "x"))
+RING_X = (("direct", "z"), ("ring", "x"))
+THEN_X = (("direct", "z"), ("direct", "x"))
+THEN_Z = (("direct", "x"), ("direct", "z"))
+GATHERS = (RING_X, THEN_Z, RING_X, RING_X, RING_X, RING_X, THEN_Z, THEN_X)
 GROUP = 4
 CODE_POWER, CODE_STEEP, CODE_LOW = 36, 120.0, 2.0**-3.45
 RULER = 320
@@ -30,9 +34,9 @@
         for side in range(SIDES):
             split = X_STRIPS[side]
             if k < split:
-                found.append((k, side, X_FIRST))
+                found.append((k, side, (X_FIRST, GATHERS[len(found)])))
             if STRIPS - 1 - k >= split:
-                found.append((STRIPS - 1 - k, side, Z_FIRST))
+                found.append((STRIPS - 1 - k, side, (Z_FIRST, GATHERS[len(found)])))
     return found
 
 
@@ -50,27 +54,37 @@
         self.now, self.free, self.heap, self.waits = 0.0, {}, [], 0
         self.sent = {}
 
-    def send(self, unit, axis, copies, arriving, then):
+    def send(self, unit, copies, arriving, then):
         k = self.waits
         self.waits += 1
         latest = 0.0
-        for delta, src, dst in copies:
+        for distances, src, dst in copies:
             pltpu.make_async_remote_copy(
                 src_ref=src,
                 dst_ref=dst,
                 send_sem=self.send_sems.at[unit],
                 recv_sem=self.recv_sems.at[k],
-                device_id={axis: wrapped(lax.axis_index(axis) + delta, SIZE[axis])},
+                device_id={axis: wrapped(lax.axis_index(axis) + d, SIZE[axis]) for axis, d in distances.items()},
                 device_id_type=MESH,
             ).start()
-            hops = abs(delta)
             size = math.prod(dst.shape) * jnp.dtype(dst.dtype).itemsize
             self.sent[unit] = self.sent.get(unit, 0) + size
-            link = (axis, delta > 0)
-            end = max(self.now, self.free.get(link, 0.0)) + hops * size / BYTES_PER_US
-            self.free[link] = end
+            end = self.now
+            for axis, d in distances.items():
+                link = (axis, d > 0)
+                self.free[link] = max(self.now, self.free.get(link, 0.0)) + abs(d) * size / BYTES_PER_US
+                end = max(end, self.free[link])
+            hops = sum(abs(d) for d in distances.values())
             latest = max(latest, end + HOP_US + FURTHER_US * (hops - 1))
         heapq.heappush(self.heap, (latest, k, arriving, then))
+
+    def room(self, size):
+        row = math.prod(self.ruler.shape[1:]) * jnp.dtype(self.ruler.dtype).itemsize
+        assert size % row == 0 and size // row <= self.ruler.shape[0]
+        return self.ruler.at[pl.ds(0, size // row)]
+
+    def span(self, *refs):
+        return self.room(sum(math.prod(ref.shape) * jnp.dtype(ref.dtype).itemsize for ref in refs))
 
     def run(self):
         while self.heap:
@@ -79,9 +93,7 @@
             pltpu.make_async_copy(arriving, arriving, self.recv_sems.at[k]).wait()
             then()
         for unit, size in self.sent.items():
-            row = math.prod(self.ruler.shape[1:]) * jnp.dtype(self.ruler.dtype).itemsize
-            assert size % row == 0 and size // row <= self.ruler.shape[0]
-            total = self.ruler.at[pl.ds(0, size // row)]
+            total = self.room(size)
             pltpu.make_async_copy(total, total, self.send_sems.at[unit]).wait()
 
 
@@ -117,44 +129,14 @@
         add_into(part.at[me], *(slots.at[i] for i in range(n - 1)))
         done(part.at[me])
 
-    copies = [(delta, part.at[wrapped(me + delta, n)], slots.at[i]) for i, delta in enumerate(deltas_of(n))]
-    flow.send(unit, axis, copies, slots, arrived)
-
-
-def reduce_ring(flow, unit, axis, part, slots, done):
-    n = SIZE[axis]
-    me = lax.axis_index(axis)
-    steps = n // 2
-    middle = part.shape[1] // 2
-    left = [2]
-
-    def advance(sign, step):
-        slot = slots.at[step if sign > 0 else steps + step]
-        chunk = part.at[wrapped(me + sign * (steps - step), n)]
-        nearer = part.at[wrapped(me + sign * (steps - step - 1), n)]
-        if step == 0:
-            half = pl.ds(0 if sign > 0 else middle, middle)
-            slot, chunk, nearer = slot.at[pl.ds(0, middle)], chunk.at[half], nearer.at[half]
-
-        def arrived():
-            add_into(nearer, slot)
-            if step + 1 < steps:
-                advance(sign, step + 1)
-                return
-            left[0] -= 1
-            if left[0] == 0:
-                done(part.at[me])
-
-        flow.send(unit, axis, [(sign, chunk, slot)], slot, arrived)
-
-    advance(1, 0)
-    advance(-1, 0)
+    copies = [({axis: d}, part.at[wrapped(me + d, n)], slots.at[i]) for i, d in enumerate(deltas_of(n))]
+    flow.send(unit, copies, slots, arrived)
 
 
 def gather_direct(flow, unit, axis, block_at, at, done):
     mine = block_at({**at, axis: lax.axis_index(axis)})
     deltas = deltas_of(SIZE[axis])
-    flow.send(unit, axis, [(delta, mine, mine) for delta in deltas], block_at(at, 0, len(deltas)), done)
+    flow.send(unit, [({axis: d}, mine, mine) for d in deltas], flow.span(*[mine] * len(deltas)), done)
 
 
 def gather_ring(flow, unit, axis, block_at, at, done):
@@ -175,7 +157,7 @@
             if left[0] == 0:
                 done()
 
-        flow.send(unit, axis, [(sign, block, block)], block, arrived)
+        flow.send(unit, [({axis: sign}, block, block)], block, arrived)
 
     advance(1, 0)
     advance(-1, 0)
@@ -265,13 +247,13 @@
                 done(part.at[me])
 
         write_code(chunk, source)
-        flow.send(unit, axis, [(sign, source, target)], target, arrived)
+        flow.send(unit, [({axis: sign}, source, target)], target, arrived)
 
     advance(1, 0)
     advance(-1, 0)
 
 
-REDUCE = {"ring": reduce_ring, "direct": reduce_direct, "coded": reduce_coded}
+REDUCE = {"direct": reduce_direct, "coded": reduce_coded}
 GATHER = {"ring": gather_ring, "direct": gather_direct}
 
 
@@ -280,9 +262,9 @@
     height, width = LEAF
     extent = SIZE["z"] * width
 
-    def block_at(at, half=0, count=None):
-        x = at.get("x", pl.ds(0, count or SIZE["x"]))
-        cols = pl.ds(side * extent, count * width if count else extent)
+    def block_at(at, half=0):
+        x = at.get("x", pl.ds(0, SIZE["x"]))
+        cols = pl.ds(side * extent, extent)
         if "z" in at:
             cols = pl.ds(pl.multiple_of(side * extent + at["z"] * width, width), width)
         if half and "z" in at:
@@ -300,8 +282,6 @@
     def reduce(k, chunk):
         if k < len(reduce_plan):
             kind, axis = reduce_plan[k]
-            if SIZE[axis] == 2:
-                kind = "direct"
             REDUCE[kind](flow, number, axis, chunk, slots[k], lambda mine: reduce(k + 1, mine))
             return
         own = block_at({axis: lax.axis_index(axis) for axis in ("x", "z")})

time: 53.4 us -> 49.6 us (0.929)
  the two profiles are of different devices: /device:TPU:16 before, /device:TPU:58 now
where the time goes in v4:
time: 49.6 us; the launch traced here: 49.5 us
  Pallas kernels  48.5 us (98%)
  local copies, waits for them, and re-layouts  0.97 us (2%)
    pallas_call x1, Pallas kernels, local(): pl.pallas_call(lambda *refs: kernel(replicas, *refs), out_shape=pltpu.VME...  48.5 us

profile of v4, /device:TPU:58, one launch (start us, length us, event | category | flops | bytes accessed | tf_op | source)
XLA Modules:
  0.0 49.5 jit_solution(1215084460219896240)
XLA Ops:
  0.0 48.5 %grad_sum.1 = bf16[4,4,16,2048]{3,2,1,0:T(8,128)(2,1)S(1)} custom-call(bf16[768,512]{1,0:T(8,128)(2,1)} %refs_0_.1, bf16[768,2048]{1,0:T(8,128)(2,1)} %refs_1_.1), custom_call_target="tpu_custom_call" | custom-call | tf_op jit(solution)/shard_map/grad_sum/pallas_call | solution.py:413
  48.5 1.0 %copy.4 = bf16[256,2048]{1,0:T(8,128)(2,1)} copy(bf16[256,2048]{1,0:T(8,128)(2,1)S(1)} %bitcast.1) | data formatting | bytes 2097152

commit v5 on v4

--- a/solution.py
+++ b/solution.py
@@ -25,7 +25,7 @@
 CODE_POWER, CODE_STEEP, CODE_LOW = 36, 120.0, 2.0**-3.45
 RULER = 320
 BYTES_PER_US = 46600.0
-HOP_US, FURTHER_US, TASK_US = 2.65, 0.9, 0.15
+HOP_US, FURTHER_US, TASK_US = 3.0, 0.9, 0.15
 
 
 def units():
@@ -118,7 +118,7 @@
 
 
 def deltas_of(n):
-    return [d for far in range(1, n // 2 + 1) for d in ((far, -far) if 2 * far < n else (far,))]
+    return [d for far in range(n // 2, 0, -1) for d in ((far, -far) if 2 * far < n else (far,))]
 
 
 def reduce_direct(flow, unit, axis, part, slots, done):

time: 49.6 us -> 49.2 us (level)
  the two profiles are of different devices: /device:TPU:58 before, /device:TPU:16 now
where the time goes in v5:
time: 49.2 us; the launch traced here: 49.1 us
  Pallas kernels  48.1 us (98%)
  local copies, waits for them, and re-layouts  0.97 us (2%)
    pallas_call x1, Pallas kernels, local(): pl.pallas_call(lambda *refs: kernel(replicas, *refs), out_shape=pltpu.VME...  48.1 us

profile of v5, /device:TPU:16, one launch (start us, length us, event | category | flops | bytes accessed | tf_op | source)
XLA Modules:
  0.0 49.1 jit_solution(13781925227930962677)
XLA Ops:
  0.0 48.1 %grad_sum.1 = bf16[4,4,16,2048]{3,2,1,0:T(8,128)(2,1)S(1)} custom-call(bf16[768,512]{1,0:T(8,128)(2,1)} %refs_0_.1, bf16[768,2048]{1,0:T(8,128)(2,1)} %refs_1_.1), custom_call_target="tpu_custom_call" | custom-call | tf_op jit(solution)/shard_map/grad_sum/pallas_call | solution.py:413
  48.2 1.0 %copy.4 = bf16[256,2048]{1,0:T(8,128)(2,1)} copy(bf16[256,2048]{1,0:T(8,128)(2,1)S(1)} %bitcast.1) | data formatting | bytes 2097152

commit v6 on v5

--- a/solution.py
+++ b/solution.py
@@ -371,7 +371,7 @@
     multiply_z(wrapped(me["z"] + SIZE["z"] // 2, SIZE["z"]))
     multiply_x(wrapped(me["x"] + SIZE["x"] // 2, SIZE["x"]))
     pl.semaphore_wait(barrier, peers)
-    for number, unit in enumerate(work):
+    for number, unit in sorted(enumerate(work), key=lambda entry: entry[1][2][0] != Z_FIRST):
         start_unit(flow, number, unit, parts[number], slots[number], out, replicas)
     for far in range(SIZE["z"] // 2 - 1, 0, -1):
         if far < SIZE["x"] // 2:

time: 49.2 us -> 48.7 us (0.990)
  Pallas kernels: 48.1 us -> 47.5 us
    pallas_call x1, Pallas kernels: 48.1 us -> 47.5 us  [local(): pl.pallas_call(lambda *refs: kernel(replicas, *refs), out_shape=pltpu.VME...]
where the time goes in v6:
time: 48.7 us; the launch traced here: 48.5 us
  Pallas kernels  47.5 us (98%)
  local copies, waits for them, and re-layouts  0.97 us (2%)
    pallas_call x1, Pallas kernels, local(): pl.pallas_call(lambda *refs: kernel(replicas, *refs), out_shape=pltpu.VME...  47.5 us

profile of v6, /device:TPU:16, one launch (start us, length us, event | category | flops | bytes accessed | tf_op | source)
XLA Modules:
  0.0 48.5 jit_solution(1141219808524328513)
XLA Ops:
  0.0 47.5 %grad_sum.1 = bf16[4,4,16,2048]{3,2,1,0:T(8,128)(2,1)S(1)} custom-call(bf16[768,512]{1,0:T(8,128)(2,1)} %refs_0_.1, bf16[768,2048]{1,0:T(8,128)(2,1)} %refs_1_.1), custom_call_target="tpu_custom_call" | custom-call | tf_op jit(solution)/shard_map/grad_sum/pallas_call | solution.py:413
  47.5 1.0 %copy.4 = bf16[256,2048]{1,0:T(8,128)(2,1)} copy(bf16[256,2048]{1,0:T(8,128)(2,1)S(1)} %bitcast.1) | data formatting | bytes 2097152
